TPU v7x, 32 devices: a whole 2x2x4 slice. The times are simulated.
32 devices in a mesh: groups: 2 (over x), win: 16 (over z, y, core).
Axes of the slice: x: 2, y: 2, z: 4, core: 2. Of those that a mesh axis runs over, the one named last changes fastest.
Arguments:
- latents: bfloat16 [6, 8, 256, 1536], P('groups', None, 'win'), parts along dimension 0, may hold values from -60 to 60
- offsets: int32 [6], P('groups'), parts along dimension 0, may hold values from 0 to 8, as said below
- levels: int32 [6], P('groups'), parts along dimension 0, may hold values from 0 to 31
- mod_table: bfloat16 [32, 6, 1536], replicated, may hold values from -3 to 3
- rel_bias: float32 [6, 64, 64], replicated, may hold values from -3 to 403
- w_qkv: bfloat16 [1536, 2304], P('win'), may hold values from -0.15625 to 0.15625
- w_out: bfloat16 [768, 1536], P('win'), may hold values from -0.21875 to 0.21875
- w_up: bfloat16 [1536, 3072], P('win'), may hold values from -0.15625 to 0.15625
- w_down: bfloat16 [3072, 1536], P('win'), may hold values from -0.109375 to 0.109375
Outputs:
- result: bfloat16 [6, 8, 256, 1536], P('groups', None, 'win'), parts along dimension 0
There are 2 independent parts, one for each index of `groups`. A program takes and returns all parts, laid end to end along the dimension named above; an argument that names none is the same for every part. Nothing has to cross between parts.
Inputs may be any that keep to these rules, and one draw needn't show every extreme that they name: `offsets`: some micro-batch has offset 8 in every draw.
All inputs are finite; a program needn't handle non-finite values.
Results may differ from a plain program's by a relative error of at most 0.007.
Values may be sent and summed in bfloat16 or wider, within the bound.
No kernel may reach another device: no remote copies, remote signals or barrier semaphores. Data moves between devices by JAX's collectives and lax.ppermute only.
A program may use at most 128 MiB of HBM per device.

v0:
```python
import jax
import jax.numpy as jnp
from jax import lax
from jax.sharding import PartitionSpec as P

HEADS = 6
HEAD_DIM = 128
WIN = 8
LEVELS = 32


def passed_along(shard, axis, by):
    length = lax.axis_size(axis)
    return lax.ppermute(shard, axis, [(i, (i + by) % length) for i in range(length)])


def norm_rows(values_in):
    centre = values_in - jnp.mean(values_in, axis=-1, keepdims=True)
    spread = jnp.mean(centre * centre, axis=-1, keepdims=True)
    return centre * lax.rsqrt(spread + 1e-06)


def restore_grid(region, arrived, offsets, columns):
    widened = jnp.concatenate([region, arrived], axis=2)
    return jax.vmap(lambda plane, shift_by: lax.dynamic_slice_in_dim(plane, shift_by, columns, 1))(
        widened, offsets
    )


def local(latents, offsets, levels, mod_table, rel_bias, w_qkv, w_out, w_up, w_down):
    batches, lat_rows, columns, features = latents.shape
    inner = HEADS * HEAD_DIM
    per_dev = columns // WIN
    selector = (levels[:, None] == jnp.arange(LEVELS, dtype=jnp.int32)[None, :]).astype(
        jnp.bfloat16
    )
    modulation = jnp.dot(
        selector, mod_table.reshape(LEVELS, 6 * features), preferred_element_type=jnp.float32
    )
    modulation = modulation.reshape(batches, 6, 1, 1, features)
    stream = latents.astype(jnp.float32)
    normed = (norm_rows(stream) * (1.0 + modulation[:, 0]) + modulation[:, 1]).astype(jnp.bfloat16)
    arrived = passed_along(normed[:, :, columns - WIN :, :], "win", 1)
    widened = jnp.concatenate([arrived, normed], axis=2)
    rolled = jax.vmap(
        lambda plane, shift_by: lax.dynamic_slice_in_dim(plane, WIN - shift_by, columns, 1)
    )(widened, offsets)
    full_qkv = lax.all_gather(w_qkv, "win", axis=0, tiled=True)
    windows = rolled.reshape(batches, lat_rows, per_dev, WIN, features).transpose(0, 2, 1, 3, 4)
    windows = windows.reshape(-1, lat_rows * WIN, features)
    number = windows.shape[0]
    triple = jnp.dot(windows.reshape(-1, features), full_qkv, preferred_element_type=jnp.float32)
    triple = triple.astype(jnp.bfloat16).reshape(number, lat_rows * WIN, 3, HEADS, HEAD_DIM)
    scores = jnp.einsum(
        "wqhe,wkhe->whqk", triple[:, :, 0], triple[:, :, 1], preferred_element_type=jnp.float32
    )
    scores = scores * (1.0 / HEAD_DIM**0.5) + rel_bias[None]
    probs = jax.nn.softmax(scores, axis=-1).astype(jnp.bfloat16)
    attended = jnp.einsum(
        "whqk,wkhe->wqhe", probs, triple[:, :, 2], preferred_element_type=jnp.float32
    ).astype(jnp.bfloat16)
    attended = attended.reshape(batches, per_dev, lat_rows, WIN, inner).transpose(0, 2, 1, 3, 4)
    attended = attended.reshape(batches, lat_rows, columns, inner)
    full_out = lax.all_gather(w_out, "win", axis=0, tiled=True)
    returned = passed_along(attended[:, :, :WIN, :], "win", -1)
    restored = restore_grid(attended, returned, offsets, columns)
    projected = jnp.dot(restored.reshape(-1, inner), full_out, preferred_element_type=jnp.float32)
    projected = projected.reshape(batches, lat_rows, columns, features)
    middle = (stream + modulation[:, 2] * projected).astype(jnp.bfloat16)
    second = (
        norm_rows(middle.astype(jnp.float32)) * (1.0 + modulation[:, 3]) + modulation[:, 4]
    ).astype(jnp.bfloat16)
    full_up = lax.all_gather(w_up, "win", axis=0, tiled=True)
    hidden = jnp.dot(second.reshape(-1, features), full_up, preferred_element_type=jnp.float32)
    hidden = jax.nn.gelu(hidden, approximate=False).astype(jnp.bfloat16)
    full_down = lax.all_gather(w_down, "win", axis=0, tiled=True)
    lowered = jnp.dot(hidden, full_down, preferred_element_type=jnp.float32).reshape(
        batches, lat_rows, columns, features
    )
    return (middle.astype(jnp.float32) + modulation[:, 5] * lowered).astype(jnp.bfloat16)


def solution(mesh):
    in_specs = (
        P("groups", None, "win", None),
        P("groups"),
        P("groups"),
        P(),
        P(),
        P("win", None),
        P("win", None),
        P("win", None),
        P("win", None),
    )
    out_specs = P("groups", None, "win", None)
    return jax.shard_map(local, mesh=mesh, in_specs=in_specs, out_specs=out_specs, check_vma=False)
```

profile of v0, /device:TPU:0, one launch (start us, length us, event | category | flops | bytes accessed | tf_op | source)
XLA Modules:
  0.0 319.7 jit_solution(2629307609174419920)
XLA Ops:
  6.5 0.0 copy-start
  6.5 0.0 copy-start.1
  6.5 0.0 all-gather.5.cloned.1.call-start
  6.5 0.7 all-gather.5.cloned.1.call-update
  7.3 0.0 all-gather.7.cloned.1.call-start
  7.3 0.7 all-gather.7.cloned.1.call-update
  8.0 0.0 all-gather.11.cloned.1.call-start
  8.1 0.7 all-gather.11.cloned.1.call-update
  8.7 0.0 all-gather.9.cloned.1.call-start
  8.8 0.5 all-gather.9.cloned.1.call-update
  9.3 0.0 copy-done
  9.3 0.9 convolution_bitcast_fusion
  10.2 0.0 copy-done.1
  10.2 0.2 convert_reduce_fusion.1
  10.5 0.4 fusion.22
  10.9 0.0 copy-start.6
  11.0 0.7 slice_bitcast_fusion.1
  11.6 0.7 fusion.25
  12.3 0.9 slice.55
  13.2 0.5 collective-permute-start
  13.7 1.7 copy.24
  15.4 0.0 copy-done.6
  15.4 11.6 %collective-permute-done = bf16[3,8,8,1536]{3,2,1,0:T(8,128)(2,1)S(1)} collective-permute-done((bf16[3,8,8,1536]{3,2,1,0:T(8,128)(2,1)}, bf16[3,8,8,1536]{3,2,1,0:T(8,128)(2,1)S(1)}, u32[]{:S(2)}, u32[]{:S(2)}) %collective-permute-start) | collective-permute-done | bytes 589856 | tf_op jit(solution)/shard_map/ppermute | solution.py:14
  27.0 0.1 pad_maximum_fusion
  27.2 0.5 copy.19
  27.7 1.7 gather_fusion
  29.4 2.7 copy.20
  32.0 48.4 %all-gather.5.cloned.1.call-done = bf16[1536,2304]{1,0:T(8,128)(2,1)} async-done(((bf16[96,2304]{1,0:T(8,128)(2,1)}), bf16[1536,2304]{1,0:T(8,128)(2,1)}) %all-gather.5.cloned.1.call-update) | async-done | bytes 7077904 | tf_op jit(solution)/shard_map/all_gather | solution.py:48
  80.5 6.3 %convolution_convert_fusion = bf16[384,2304]{1,0:T(8,128)(2,1)S(1)} fusion(bf16[384,1536]{1,0:T(8,128)(2,1)} %bitcast.93, bf16[1536,2304]{1,0:T(8,128)(2,1)} %all-gather.5.cloned.1.call-done), kind=kOutput, calls=%fused_computation.22 | convolution fusion | flops 2718793728 | bytes 10027008 | tf_op jit(solution)/shard_map/dot_general | solution.py:52
  86.7 3.1 reshape.85
  89.9 0.0 copy-start.2
  89.9 2.9 fusion.109
  92.8 0.0 copy-done.2
  92.8 0.4 fusion.60
  93.3 0.3 fusion.110
  93.6 2.5 fusion.61
  96.0 1.5 copy.26
  97.5 0.7 reshape.86
  98.2 0.1 copy.27
  98.3 2.2 collective-permute-start.1
  100.6 4.2 %collective-permute-done.1 = bf16[3,8,8,768]{3,1,0,2:T(8,128)(2,1)S(1)} collective-permute-done((bf16[3,8,8,768]{3,1,0,2:T(8,128)(2,1)S(1)}, bf16[3,8,8,768]{3,1,0,2:T(8,128)(2,1)S(1)}, u32[]{:S(2)}, u32[]{:S(2)}) %collective-permute-start.1) | collective-permute-done | bytes 294944 | tf_op jit(solution)/shard_map/ppermute | solution.py:14
  104.8 0.1 pad_maximum_fusion.1
  104.9 0.6 gather_fusion.1
  105.5 18.4 %all-gather.7.cloned.1.call-done = bf16[768,1536]{1,0:T(8,128)(2,1)} async-done(((bf16[48,1536]{1,0:T(8,128)(2,1)}), bf16[768,1536]{1,0:T(8,128)(2,1)}) %all-gather.7.cloned.1.call-update) | async-done | bytes 2359312 | tf_op jit(solution)/shard_map/all_gather | solution.py:64
  123.9 0.0 copy-start.4
  123.9 0.0 copy-start.5
  123.9 2.9 convert_reduce_fusion
  126.8 0.4 fusion.18
  127.2 0.0 copy-done.4
  127.2 0.0 copy-done.5
  127.2 0.7 fusion.21
  127.9 77.9 %all-gather.11.cloned.1.call-done = bf16[3072,1536]{1,0:T(8,128)(2,1)} async-done(((bf16[192,1536]{1,0:T(8,128)(2,1)}), bf16[3072,1536]{1,0:T(8,128)(2,1)}) %all-gather.11.cloned.1.call-update) | async-done | bytes 9437200 | tf_op jit(solution)/shard_map/all_gather | solution.py:76
  205.8 81.5 %all-gather.9.cloned.1.call-done = bf16[1536,3072]{1,0:T(8,128)(2,1)} async-done(((bf16[96,3072]{1,0:T(8,128)(2,1)}), bf16[1536,3072]{1,0:T(8,128)(2,1)}) %all-gather.9.cloned.1.call-update) | async-done | bytes 9437200 | tf_op jit(solution)/shard_map/all_gather | solution.py:73
  287.3 0.0 copy-start.3
  287.3 22.8 %fusion.16 = f32[384,1536]{1,0:T(8,128)} fusion(bf16[3072,1536]{1,0:T(8,128)(2,1)} %all-gather.11.cloned.1.call-done, bf16[384,1536]{1,0:T(8,128)(2,1)S(1)} %bitcast.92, bf16[1536,3072]{1,0:T(8,128)(2,1)} %all-gather.9.cloned.1.call-done), kind=kOutput, calls=%fused_computation.35 | convolution fusion | flops 7324434432 | bytes 22413312 | tf_op jit(solution)/shard_map/dot_general | solution.py:77
  310.1 0.0 copy-done.3
  310.1 3.1 fusion.26
  (6 shorter events, 0.1 us)
Async XLA Ops:
  6.5 2.8 copy-start
  6.5 3.7 %copy-start.1 = (bf16[3,8,16,1536]{3,2,1,0:T(8,128)(2,1)S(1)}, bf16[3,8,16,1536]{3,2,1,0:T(8,128)(2,1)}, u32[]{:S(2)}) copy-start(bf16[3,8,16,1536]{3,2,1,0:T(8,128)(2,1)} %param.9) | copy-start | bytes 3538948
  6.5 73.9 %all-gather.5.cloned.1.call-start = ((), (), s32[]{:S(2)}) async-start(), calls=%async_computation | async-start | bytes 7520256 | tf_op jit(solution)/shard_map/all_gather | solution.py:48
  7.3 116.6 %all-gather.7.cloned.1.call-start = ((), (), s32[]{:S(2)}) async-start(), calls=%async_computation.1 | async-start | bytes 2506752 | tf_op jit(solution)/shard_map/all_gather | solution.py:64
  8.0 197.8 %all-gather.11.cloned.1.call-start = ((), (), s32[]{:S(2)}) async-start(), calls=%async_computation.3 | async-start | bytes 10027008 | tf_op jit(solution)/shard_map/all_gather | solution.py:76
  8.7 278.5 %all-gather.9.cloned.1.call-start = ((), (), s32[]{:S(2)}) async-start(), calls=%async_computation.2 | async-start | bytes 10027008 | tf_op jit(solution)/shard_map/all_gather | solution.py:73
  10.9 4.5 %copy-start.6 = (s32[3]{0:T(128)S(1)}, s32[3]{0:T(128)}, u32[]{:S(2)}) copy-start(s32[3]{0:T(128)} %param.10) | copy-start | bytes 40
  13.2 13.9 %collective-permute-start = (bf16[3,8,8,1536]{3,2,1,0:T(8,128)(2,1)}, bf16[3,8,8,1536]{3,2,1,0:T(8,128)(2,1)S(1)}, u32[]{:S(2)}, u32[]{:S(2)}) collective-permute-start(bf16[3,8,8,1536]{3,2,1,0:T(8,128)(2,1)} %slice.55), channel_id=1, source_target_pairs={{0,1},{1,2},{2,3},{3,4},{4,5},{5,6},{6,7},{7,8},{8,9},{9,10},{10,1... | collective-permute-start | bytes 1769480 | tf_op jit(solution)/shard_map/ppermute | solution.py:14
  89.9 2.9 copy-start.2
  98.3 6.5 %collective-permute-start.1 = (bf16[3,8,8,768]{3,1,0,2:T(8,128)(2,1)S(1)}, bf16[3,8,8,768]{3,1,0,2:T(8,128)(2,1)S(1)}, u32[]{:S(2)}, u32[]{:S(2)}) collective-permute-start(bf16[3,8,8,768]{3,1,0,2:T(8,128)(2,1)S(1)} %slice.59), channel_id=1, source_target_pairs={{0,15},{1,0},{2,1},{3,2},{4,3},{5,4},{6,5},{7,6},{8,7},{9,8},{10,9... | collective-permute-start | bytes 884744 | tf_op jit(solution)/shard_map/ppermute | solution.py:14
  123.9 3.4 %copy-start.4 = (f32[3,1536]{1,0:T(4,128)S(1)}, f32[3,1536]{1,0:T(4,128)}, u32[]{:S(2)}) copy-start(f32[3,1536]{1,0:T(4,128)} %get-tuple-element.9) | copy-start | bytes 55300
  123.9 3.4 %copy-start.5 = (f32[3,1536]{1,0:T(4,128)S(1)}, f32[3,1536]{1,0:T(4,128)}, u32[]{:S(2)}) copy-start(f32[3,1536]{1,0:T(4,128)} %get-tuple-element.10) | copy-start | bytes 55300
  287.3 22.9 %copy-start.3 = (f32[3,1536]{1,0:T(4,128)S(1)}, f32[3,1536]{1,0:T(4,128)}, u32[]{:S(2)}) copy-start(f32[3,1536]{1,0:T(4,128)} %get-tuple-element.8) | copy-start | bytes 55300
Sparse Core Ops, SparseCore 0:
  9.6 70.7 all-gather.4
  82.7 41.0 all-gather.6
  126.1 79.6 all-gather.10
  207.9 79.3 all-gather.8
where the time goes:
time: 320 us
  waiting for transfers between devices  245 us (77%)
  matrix products  35.8 us (11%)
  local copies, waits for them, and re-layouts  16.4 us (5%)
  between operations  13.3 us (4%)
  other arithmetic  6.74 us (2%)
    all_gather x1, waiting for transfers between devices, local(): full_up = lax.all_gather(w_up, 'win', axis=0, tiled=True)  81.5 us
    all_gather x1, waiting for transfers between devices, local(): full_down = lax.all_gather(w_down, 'win', axis=0, tiled=True)  77.9 us
    all_gather x1, waiting for transfers between devices, local(): full_qkv = lax.all_gather(w_qkv, 'win', axis=0, tiled=True)  48.4 us
    dot_general x1, matrix products, local(): jnp.dot(hidden, full_down, preferred_element_type=jnp.float32)  22.8 us
    all_gather x1, waiting for transfers between devices, local(): full_out = lax.all_gather(w_out, 'win', axis=0, tiled=True)  18.4 us
    ppermute x2, waiting for transfers between devices, passed_along(): lax.ppermute(shard, axis, [(i, (i + by) % length) for i in range(length)])  15.9 us
  transfers between devices with their start and end apart: 6, of which 6 were waited for; matrix products, arithmetic and copies ran while one was open for 10% of the time, Pallas kernels for 0%

commit v1 on v0

--- a/solution.py
+++ b/solution.py
@@ -70,7 +70,12 @@
     second = (
         norm_rows(middle.astype(jnp.float32)) * (1.0 + modulation[:, 3]) + modulation[:, 4]
     ).astype(jnp.bfloat16)
-    full_up = lax.all_gather(w_up, "win", axis=0, tiled=True)
+    ring = [w_up]
+    for hop in range(15):
+        ring.append(lax.ppermute(ring[-1], "win", [(dev, (dev + 1) % 16) for dev in range(16)]))
+    full_up = jnp.roll(
+        jnp.concatenate(ring[::-1], axis=0), (lax.axis_index("win") + 1) * ring[0].shape[0], axis=0
+    )
     hidden = jnp.dot(second.reshape(-1, features), full_up, preferred_element_type=jnp.float32)
     hidden = jax.nn.gelu(hidden, approximate=False).astype(jnp.bfloat16)
     full_down = lax.all_gather(w_down, "win", axis=0, tiled=True)

time: 320 us -> 380 us (1.19)
  local copies, waits for them, and re-layouts: 16.4 us -> 56.4 us
  waiting for transfers between devices: 245 us -> 262 us
    ppermute x0 -> x15, waiting for transfers between devices: none -> 244 us  [local(): lax.ppermute(ring[-1], 'win', [(dev, (dev + 1) % 16) for dev in range(16)])]
    all_gather x1 -> x0, waiting for transfers between devices: 81.5 us -> none  [local(): full_up = lax.all_gather(w_up, 'win', axis=0, tiled=True)]
    all_gather x1, waiting for transfers between devices: 77.9 us -> 0.02 us  [local(): full_down = lax.all_gather(w_down, 'win', axis=0, tiled=True)]
    all_gather x1, waiting for transfers between devices: 48.4 us -> 0.01 us  [local(): full_qkv = lax.all_gather(w_qkv, 'win', axis=0, tiled=True)]
    unnamed x15 -> x102, local copies, waits for them, and re-layouts: 1.76 us -> 41.8 us
    all_gather x1, waiting for transfers between devices: 18.4 us -> 0.02 us  [local(): full_out = lax.all_gather(w_out, 'win', axis=0, tiled=True)]
  transfers between devices with their start and end apart: 6 -> 20, of which waited for: 6 -> 17; matrix products, arithmetic and copies ran while one was open for 10% -> 18% of each run, Pallas kernels for 0% -> 0%
where the time goes in v1:
time: 380 us; the launch traced here: 379 us
  waiting for transfers between devices  262 us (69%)
  local copies, waits for them, and re-layouts  56.4 us (15%)
  matrix products  36.1 us (10%)
  between operations  13.4 us (4%)
  other arithmetic  10.1 us (3%)
    ppermute x15, waiting for transfers between devices, local(): lax.ppermute(ring[-1], 'win', [(dev, (dev + 1) % 16) for dev in range(16)])  244 us
    unnamed x102, local copies, waits for them, and re-layouts  41.8 us
    dot_general x1, matrix products, local(): jnp.dot(hidden, full_down, preferred_element_type=jnp.float32)  24 us
    ppermute x2, waiting for transfers between devices, passed_along(): lax.ppermute(shard, axis, [(i, (i + by) % length) for i in range(length)])  17.1 us
  transfers between devices with their start and end apart: 20, of which 17 were waited for; matrix products, arithmetic and copies ran while one was open for 18% of the time, Pallas kernels for 0%

profile of v1, /device:TPU:0, one launch (start us, length us, event | category | flops | bytes accessed | tf_op | source)
XLA Modules:
  0.0 379.1 jit_solution(14538247487455385234)
XLA Ops:
  7.9 12.8 %collective-permute-done.2 = bf16[96,3072]{1,0:T(8,128)(2,1)S(1)} collective-permute-done((bf16[96,3072]{1,0:T(8,128)(2,1)}, bf16[96,3072]{1,0:T(8,128)(2,1)S(1)}, u32[]{:S(2)}, u32[]{:S(2)}) %collective-permute-start.2) | collective-permute-done | bytes 589856 | tf_op jit(solution)/shard_map/ppermute | solution.py:75
  21.4 24.5 %collective-permute-done.3 = bf16[96,3072]{1,0:T(8,128)(2,1)S(1)} collective-permute-done((bf16[96,3072]{1,0:T(8,128)(2,1)S(1)}, bf16[96,3072]{1,0:T(8,128)(2,1)S(1)}, u32[]{:S(2)}, u32[]{:S(2)}) %collective-permute-start.3) | collective-permute-done | bytes 589856 | tf_op jit(solution)/shard_map/ppermute | solution.py:75
  46.8 20.7 %collective-permute-done.4 = bf16[96,3072]{1,0:T(8,128)(2,1)S(1)} collective-permute-done((bf16[96,3072]{1,0:T(8,128)(2,1)S(1)}, bf16[96,3072]{1,0:T(8,128)(2,1)S(1)}, u32[]{:S(2)}, u32[]{:S(2)}) %collective-permute-start.4) | collective-permute-done | bytes 589856 | tf_op jit(solution)/shard_map/ppermute | solution.py:75
  67.6 24.7 %collective-permute-done.5 = bf16[96,3072]{1,0:T(8,128)(2,1)S(1)} collective-permute-done((bf16[96,3072]{1,0:T(8,128)(2,1)S(1)}, bf16[96,3072]{1,0:T(8,128)(2,1)S(1)}, u32[]{:S(2)}, u32[]{:S(2)}) %collective-permute-start.5) | collective-permute-done | bytes 589856 | tf_op jit(solution)/shard_map/ppermute | solution.py:75
  92.3 12.0 %collective-permute-done.6 = bf16[96,3072]{1,0:T(8,128)(2,1)S(1)} collective-permute-done((bf16[96,3072]{1,0:T(8,128)(2,1)S(1)}, bf16[96,3072]{1,0:T(8,128)(2,1)S(1)}, u32[]{:S(2)}, u32[]{:S(2)}) %collective-permute-start.6) | collective-permute-done | bytes 589856 | tf_op jit(solution)/shard_map/ppermute | solution.py:75
  105.1 15.2 %collective-permute-done.7 = bf16[96,3072]{1,0:T(8,128)(2,1)S(1)} collective-permute-done((bf16[96,3072]{1,0:T(8,128)(2,1)S(1)}, bf16[96,3072]{1,0:T(8,128)(2,1)S(1)}, u32[]{:S(2)}, u32[]{:S(2)}) %collective-permute-start.7) | collective-permute-done | bytes 589856 | tf_op jit(solution)/shard_map/ppermute | solution.py:75
  121.0 20.2 %collective-permute-done.8 = bf16[96,3072]{1,0:T(8,128)(2,1)S(1)} collective-permute-done((bf16[96,3072]{1,0:T(8,128)(2,1)S(1)}, bf16[96,3072]{1,0:T(8,128)(2,1)S(1)}, u32[]{:S(2)}, u32[]{:S(2)}) %collective-permute-start.8) | collective-permute-done | bytes 589856 | tf_op jit(solution)/shard_map/ppermute | solution.py:75
  142.1 12.0 %collective-permute-done.9 = bf16[96,3072]{1,0:T(8,128)(2,1)S(1)} collective-permute-done((bf16[96,3072]{1,0:T(8,128)(2,1)S(1)}, bf16[96,3072]{1,0:T(8,128)(2,1)S(1)}, u32[]{:S(2)}, u32[]{:S(2)}) %collective-permute-start.9) | collective-permute-done | bytes 589856 | tf_op jit(solution)/shard_map/ppermute | solution.py:75
  154.9 12.0 %collective-permute-done.10 = bf16[96,3072]{1,0:T(8,128)(2,1)S(1)} collective-permute-done((bf16[96,3072]{1,0:T(8,128)(2,1)S(1)}, bf16[96,3072]{1,0:T(8,128)(2,1)S(1)}, u32[]{:S(2)}, u32[]{:S(2)}) %collective-permute-start.10) | collective-permute-done | bytes 589856 | tf_op jit(solution)/shard_map/ppermute | solution.py:75
  167.7 12.0 %collective-permute-done.11 = bf16[96,3072]{1,0:T(8,128)(2,1)S(1)} collective-permute-done((bf16[96,3072]{1,0:T(8,128)(2,1)S(1)}, bf16[96,3072]{1,0:T(8,128)(2,1)S(1)}, u32[]{:S(2)}, u32[]{:S(2)}) %collective-permute-start.11) | collective-permute-done | bytes 589856 | tf_op jit(solution)/shard_map/ppermute | solution.py:75
  179.7 1.7 convert_reduce_fusion.1
  181.4 10.4 %collective-permute-done.12 = bf16[96,3072]{1,0:T(8,128)(2,1)} collective-permute-done((bf16[96,3072]{1,0:T(8,128)(2,1)S(1)}, bf16[96,3072]{1,0:T(8,128)(2,1)}, u32[]{:S(2)}, u32[]{:S(2)}) %collective-permute-start.12) | collective-permute-done | bytes 589856 | tf_op jit(solution)/shard_map/ppermute | solution.py:75
  191.8 1.7 fusion.24
  193.6 23.3 %collective-permute-done.13 = bf16[96,3072]{1,0:T(8,128)(2,1)S(1)} collective-permute-done((bf16[96,3072]{1,0:T(8,128)(2,1)}, bf16[96,3072]{1,0:T(8,128)(2,1)S(1)}, u32[]{:S(2)}, u32[]{:S(2)}) %collective-permute-start.13) | collective-permute-done | bytes 589856 | tf_op jit(solution)/shard_map/ppermute | solution.py:75
  216.8 0.9 convolution_bitcast_fusion
  218.4 11.3 %collective-permute-done.14 = bf16[96,3072]{1,0:T(8,128)(2,1)S(1)} collective-permute-done((bf16[96,3072]{1,0:T(8,128)(2,1)S(1)}, bf16[96,3072]{1,0:T(8,128)(2,1)S(1)}, u32[]{:S(2)}, u32[]{:S(2)}) %collective-permute-start.14) | collective-permute-done | bytes 589856 | tf_op jit(solution)/shard_map/ppermute | solution.py:75
  231.3 0.9 slice.55
  232.1 22.6 %collective-permute-done.15 = bf16[96,3072]{1,0:T(8,128)(2,1)} collective-permute-done((bf16[96,3072]{1,0:T(8,128)(2,1)S(1)}, bf16[96,3072]{1,0:T(8,128)(2,1)}, u32[]{:S(2)}, u32[]{:S(2)}) %collective-permute-start.15) | collective-permute-done | bytes 589856 | tf_op jit(solution)/shard_map/ppermute | solution.py:75
  254.7 1.7 copy.24
  256.4 13.7 %collective-permute-done = bf16[3,8,8,1536]{3,2,1,0:T(8,128)(2,1)S(1)} collective-permute-done((bf16[3,8,8,1536]{3,2,1,0:T(8,128)(2,1)}, bf16[3,8,8,1536]{3,2,1,0:T(8,128)(2,1)S(1)}, u32[]{:S(2)}, u32[]{:S(2)}) %collective-permute-start) | collective-permute-done | bytes 589856 | tf_op jit(solution)/shard_map/ppermute | solution.py:14
  270.9 1.7 gather_fusion
  272.5 2.8 copy.20
  275.3 10.7 %collective-permute-done.16 = bf16[96,3072]{1,0:T(8,128)(2,1)} collective-permute-done((bf16[96,3072]{1,0:T(8,128)(2,1)}, bf16[96,3072]{1,0:T(8,128)(2,1)}, u32[]{:S(2)}, u32[]{:S(2)}) %collective-permute-start.16) | collective-permute-done | bytes 589856 | tf_op jit(solution)/shard_map/ppermute | solution.py:75
  286.0 1.9 constant_dynamic-update-slice_fusion.31
  287.9 2.0 constant_dynamic-update-slice_fusion.30
  289.9 0.9 constant_dynamic-update-slice_fusion.29
  290.8 0.9 constant_dynamic-update-slice_fusion.28
  291.7 2.0 constant_dynamic-update-slice_fusion.27
  293.7 0.9 constant_dynamic-update-slice_fusion.26
  294.5 0.9 constant_dynamic-update-slice_fusion.25
  295.4 0.9 constant_dynamic-update-slice_fusion.24
  296.3 0.9 constant_dynamic-update-slice_fusion.23
  297.2 0.9 constant_dynamic-update-slice_fusion.22
  298.0 0.9 constant_dynamic-update-slice_fusion.21
  298.9 0.9 constant_dynamic-update-slice_fusion.20
  299.8 0.9 constant_dynamic-update-slice_fusion.19
  300.6 0.9 constant_dynamic-update-slice_fusion.18
  301.6 0.9 constant_dynamic-update-slice_fusion.17
  302.5 0.9 constant_dynamic-update-slice_fusion.16
  303.4 1.9 constant_dynamic-update-slice_fusion.15
  305.3 1.9 constant_dynamic-update-slice_fusion.14
  307.2 0.9 constant_dynamic-update-slice_fusion.13
  308.1 0.9 constant_dynamic-update-slice_fusion.12
  308.9 2.0 constant_dynamic-update-slice_fusion.11
  310.9 0.9 constant_dynamic-update-slice_fusion.10
  311.8 0.9 constant_dynamic-update-slice_fusion.9
  312.6 0.8 constant_dynamic-update-slice_fusion.8
  313.5 0.9 constant_dynamic-update-slice_fusion.7
  314.4 0.9 constant_dynamic-update-slice_fusion.6
  315.2 0.9 constant_dynamic-update-slice_fusion.5
  316.1 0.9 constant_dynamic-update-slice_fusion.4
  317.0 0.9 constant_dynamic-update-slice_fusion.3
  317.8 0.9 constant_dynamic-update-slice_fusion.2
  318.7 0.9 constant_dynamic-update-slice_fusion.1
  319.6 6.3 %convolution_convert_fusion = bf16[384,2304]{1,0:T(8,128)(2,1)S(1)} fusion(bf16[384,1536]{1,0:T(8,128)(2,1)} %bitcast.83, bf16[1536,2304]{1,0:T(8,128)(2,1)} %all-gather.4.cloned.1.call-done), kind=kOutput, calls=%fused_computation.24 | convolution fusion | flops 2718793728 | bytes 10027008 | tf_op jit(solution)/shard_map/dot_general | solution.py:52
  325.9 3.1 reshape.85
  329.0 2.9 fusion.117
  332.4 0.9 fusion.118
  333.3 1.6 fusion.67
  336.5 0.9 constant_dynamic-update-slice_fusion
  337.3 3.4 collective-permute-done.1
  341.4 2.9 convert_reduce_fusion
  345.5 24.0 %fusion.18 = f32[384,1536]{1,0:T(8,128)} fusion(bf16[3072,1536]{1,0:T(8,128)(2,1)} %all-gather.8.cloned.1.call-done, bf16[384,1536]{1,0:T(8,128)(2,1)S(1)} %bitcast.84, bf16[3072,3072]{1,0:T(8,128)(2,1)} %constant_dynamic-update-slice_fusion, s32[]{:T(128)S(6)} %select_n.22), kind=kOutput, calls=%fused_computation.37 | convolution fusion | flops 7324434432 | bytes 22413316 | tf_op jit(solution)/shard_map/dot_general | solution.py:82
  369.5 3.1 fusion.28
  (114 shorter events, 13.8 us)
Async XLA Ops:
  6.5 210.3 %copy-start = (bf16[32,6,1536]{2,0,1:T(8,128)(2,1)S(1)}, bf16[32,6,1536]{2,0,1:T(8,128)(2,1)}, u32[]{:S(2)}) copy-start(bf16[32,6,1536]{2,0,1:T(8,128)(2,1)} %param.12) | copy-start | bytes 1769476
  6.5 224.0 %copy-start.2 = (bf16[3,8,16,1536]{3,2,1,0:T(8,128)(2,1)S(1)}, bf16[3,8,16,1536]{3,2,1,0:T(8,128)(2,1)}, u32[]{:S(2)}) copy-start(bf16[3,8,16,1536]{3,2,1,0:T(8,128)(2,1)} %param.9) | copy-start | bytes 3538948
  6.5 249.9 %copy-start.34 = (s32[3]{0:T(128)S(1)}, s32[3]{0:T(128)}, u32[]{:S(2)}) copy-start(s32[3]{0:T(128)} %param.10) | copy-start | bytes 40
  6.5 313.0 %all-gather.4.cloned.1.call-start = ((), (), s32[]{:S(2)}) async-start(), calls=%async_computation | async-start | bytes 7520256 | tf_op jit(solution)/shard_map/all_gather | solution.py:48
  7.3 334.1 %all-gather.6.cloned.1.call-start = ((), (), s32[]{:S(2)}) async-start(), calls=%async_computation.1 | async-start | bytes 2506752 | tf_op jit(solution)/shard_map/all_gather | solution.py:64
  7.3 13.3 %collective-permute-start.2 = (bf16[96,3072]{1,0:T(8,128)(2,1)}, bf16[96,3072]{1,0:T(8,128)(2,1)S(1)}, u32[]{:S(2)}, u32[]{:S(2)}) collective-permute-start(bf16[96,3072]{1,0:T(8,128)(2,1)} %param.16), channel_id=1, source_target_pairs={{0,1},{1,2},{2,3},{3,4},{4,5},{5,6},{6,7},{7,8},{8,9},{9,10},{10,1... | collective-permute-start | bytes 1769480 | tf_op jit(solution)/shard_map/ppermute | solution.py:75
  20.6 0.8 copy-start.4
  21.4 24.5 %collective-permute-start.3 = (bf16[96,3072]{1,0:T(8,128)(2,1)S(1)}, bf16[96,3072]{1,0:T(8,128)(2,1)S(1)}, u32[]{:S(2)}, u32[]{:S(2)}) collective-permute-start(bf16[96,3072]{1,0:T(8,128)(2,1)S(1)} %collective-permute-done.2), channel_id=1, source_target_pairs={{0,1},{1,2},{2,3},{3,4},{4,5},{5,6},{6,7},{7,8},{8,9},{9,10},{10,1... | collective-permute-start | bytes 1769480 | tf_op jit(solution)/shard_map/ppermute | solution.py:75
  45.9 0.8 copy-start.6
  46.8 20.7 %collective-permute-start.4 = (bf16[96,3072]{1,0:T(8,128)(2,1)S(1)}, bf16[96,3072]{1,0:T(8,128)(2,1)S(1)}, u32[]{:S(2)}, u32[]{:S(2)}) collective-permute-start(bf16[96,3072]{1,0:T(8,128)(2,1)S(1)} %collective-permute-done.3), channel_id=1, source_target_pairs={{0,1},{1,2},{2,3},{3,4},{4,5},{5,6},{6,7},{7,8},{8,9},{9,10},{10,1... | collective-permute-start | bytes 1769480 | tf_op jit(solution)/shard_map/ppermute | solution.py:75
  67.5 162.3 %copy-start.8 = (bf16[96,3072]{1,0:T(8,128)(2,1)}, bf16[96,3072]{1,0:T(8,128)(2,1)S(1)}, u32[]{:S(2)}) copy-start(bf16[96,3072]{1,0:T(8,128)(2,1)S(1)} %collective-permute-done.4) | copy-start | bytes 1769476
  67.5 24.8 %collective-permute-start.5 = (bf16[96,3072]{1,0:T(8,128)(2,1)S(1)}, bf16[96,3072]{1,0:T(8,128)(2,1)S(1)}, u32[]{:S(2)}, u32[]{:S(2)}) collective-permute-start(bf16[96,3072]{1,0:T(8,128)(2,1)S(1)} %collective-permute-done.4), channel_id=1, source_target_pairs={{0,1},{1,2},{2,3},{3,4},{4,5},{5,6},{6,7},{7,8},{8,9},{9,10},{10,1... | collective-permute-start | bytes 1769480 | tf_op jit(solution)/shard_map/ppermute | solution.py:75
  67.5 278.0 %all-gather.8.cloned.1.call-start = ((), (), s32[]{:S(2)}) async-start(), calls=%async_computation.2 | async-start | bytes 10027008 | tf_op jit(solution)/shard_map/all_gather | solution.py:81
  92.2 137.5 %copy-start.10 = (bf16[96,3072]{1,0:T(8,128)(2,1)}, bf16[96,3072]{1,0:T(8,128)(2,1)S(1)}, u32[]{:S(2)}) copy-start(bf16[96,3072]{1,0:T(8,128)(2,1)S(1)} %collective-permute-done.5) | copy-start | bytes 1769476
  92.2 12.0 %collective-permute-start.6 = (bf16[96,3072]{1,0:T(8,128)(2,1)S(1)}, bf16[96,3072]{1,0:T(8,128)(2,1)S(1)}, u32[]{:S(2)}, u32[]{:S(2)}) collective-permute-start(bf16[96,3072]{1,0:T(8,128)(2,1)S(1)} %collective-permute-done.5), channel_id=1, source_target_pairs={{0,1},{1,2},{2,3},{3,4},{4,5},{5,6},{6,7},{7,8},{8,9},{9,10},{10,1... | collective-permute-start | bytes 1769480 | tf_op jit(solution)/shard_map/ppermute | solution.py:75
  104.3 0.8 copy-start.12
  105.1 15.2 %collective-permute-start.7 = (bf16[96,3072]{1,0:T(8,128)(2,1)S(1)}, bf16[96,3072]{1,0:T(8,128)(2,1)S(1)}, u32[]{:S(2)}, u32[]{:S(2)}) collective-permute-start(bf16[96,3072]{1,0:T(8,128)(2,1)S(1)} %collective-permute-done.6), channel_id=1, source_target_pairs={{0,1},{1,2},{2,3},{3,4},{4,5},{5,6},{6,7},{7,8},{8,9},{9,10},{10,1... | collective-permute-start | bytes 1769480 | tf_op jit(solution)/shard_map/ppermute | solution.py:75
  120.2 0.8 copy-start.14
  121.0 20.2 %collective-permute-start.8 = (bf16[96,3072]{1,0:T(8,128)(2,1)S(1)}, bf16[96,3072]{1,0:T(8,128)(2,1)S(1)}, u32[]{:S(2)}, u32[]{:S(2)}) collective-permute-start(bf16[96,3072]{1,0:T(8,128)(2,1)S(1)} %collective-permute-done.7), channel_id=1, source_target_pairs={{0,1},{1,2},{2,3},{3,4},{4,5},{5,6},{6,7},{7,8},{8,9},{9,10},{10,1... | collective-permute-start | bytes 1769480 | tf_op jit(solution)/shard_map/ppermute | solution.py:75
  141.2 0.8 copy-start.16
  142.1 12.0 %collective-permute-start.9 = (bf16[96,3072]{1,0:T(8,128)(2,1)S(1)}, bf16[96,3072]{1,0:T(8,128)(2,1)S(1)}, u32[]{:S(2)}, u32[]{:S(2)}) collective-permute-start(bf16[96,3072]{1,0:T(8,128)(2,1)S(1)} %collective-permute-done.8), channel_id=1, source_target_pairs={{0,1},{1,2},{2,3},{3,4},{4,5},{5,6},{6,7},{7,8},{8,9},{9,10},{10,1... | collective-permute-start | bytes 1769480 | tf_op jit(solution)/shard_map/ppermute | solution.py:75
  154.1 0.8 copy-start.18
  154.9 12.0 %collective-permute-start.10 = (bf16[96,3072]{1,0:T(8,128)(2,1)S(1)}, bf16[96,3072]{1,0:T(8,128)(2,1)S(1)}, u32[]{:S(2)}, u32[]{:S(2)}) collective-permute-start(bf16[96,3072]{1,0:T(8,128)(2,1)S(1)} %collective-permute-done.9), channel_id=1, source_target_pairs={{0,1},{1,2},{2,3},{3,4},{4,5},{5,6},{6,7},{7,8},{8,9},{9,10},{10,1... | collective-permute-start | bytes 1769480 | tf_op jit(solution)/shard_map/ppermute | solution.py:75
  166.9 0.8 copy-start.20
  167.7 12.0 %collective-permute-start.11 = (bf16[96,3072]{1,0:T(8,128)(2,1)S(1)}, bf16[96,3072]{1,0:T(8,128)(2,1)S(1)}, u32[]{:S(2)}, u32[]{:S(2)}) collective-permute-start(bf16[96,3072]{1,0:T(8,128)(2,1)S(1)} %collective-permute-done.10), channel_id=1, source_target_pairs={{0,1},{1,2},{2,3},{3,4},{4,5},{5,6},{6,7},{7,8},{8,9},{9,10},{10,1... | collective-permute-start | bytes 1769480 | tf_op jit(solution)/shard_map/ppermute | solution.py:75
  179.7 90.5 %copy-start.22 = (bf16[96,3072]{1,0:T(8,128)(2,1)}, bf16[96,3072]{1,0:T(8,128)(2,1)S(1)}, u32[]{:S(2)}) copy-start(bf16[96,3072]{1,0:T(8,128)(2,1)S(1)} %collective-permute-done.11) | copy-start | bytes 1769476
  179.7 12.1 %collective-permute-start.12 = (bf16[96,3072]{1,0:T(8,128)(2,1)S(1)}, bf16[96,3072]{1,0:T(8,128)(2,1)}, u32[]{:S(2)}, u32[]{:S(2)}) collective-permute-start(bf16[96,3072]{1,0:T(8,128)(2,1)S(1)} %collective-permute-done.11), channel_id=1, source_target_pairs={{0,1},{1,2},{2,3},{3,4},{4,5},{5,6},{6,7},{7,8},{8,9},{9,10},{10,1... | collective-permute-start | bytes 1769480 | tf_op jit(solution)/shard_map/ppermute | solution.py:75
  191.8 25.0 %collective-permute-start.13 = (bf16[96,3072]{1,0:T(8,128)(2,1)}, bf16[96,3072]{1,0:T(8,128)(2,1)S(1)}, u32[]{:S(2)}, u32[]{:S(2)}) collective-permute-start(bf16[96,3072]{1,0:T(8,128)(2,1)} %collective-permute-done.12), channel_id=1, source_target_pairs={{0,1},{1,2},{2,3},{3,4},{4,5},{5,6},{6,7},{7,8},{8,9},{9,10},{10,1... | collective-permute-start | bytes 1769480 | tf_op jit(solution)/shard_map/ppermute | solution.py:75
  216.8 13.0 %copy-start.24 = (bf16[96,3072]{1,0:T(8,128)(2,1)}, bf16[96,3072]{1,0:T(8,128)(2,1)S(1)}, u32[]{:S(2)}) copy-start(bf16[96,3072]{1,0:T(8,128)(2,1)S(1)} %collective-permute-done.13) | copy-start | bytes 1769476
  216.8 12.9 %collective-permute-start.14 = (bf16[96,3072]{1,0:T(8,128)(2,1)S(1)}, bf16[96,3072]{1,0:T(8,128)(2,1)S(1)}, u32[]{:S(2)}, u32[]{:S(2)}) collective-permute-start(bf16[96,3072]{1,0:T(8,128)(2,1)S(1)} %collective-permute-done.13), channel_id=1, source_target_pairs={{0,1},{1,2},{2,3},{3,4},{4,5},{5,6},{6,7},{7,8},{8,9},{9,10},{10,1... | collective-permute-start | bytes 1769480 | tf_op jit(solution)/shard_map/ppermute | solution.py:75
  229.8 0.8 copy-start.27
  229.8 24.9 %collective-permute-start.15 = (bf16[96,3072]{1,0:T(8,128)(2,1)S(1)}, bf16[96,3072]{1,0:T(8,128)(2,1)}, u32[]{:S(2)}, u32[]{:S(2)}) collective-permute-start(bf16[96,3072]{1,0:T(8,128)(2,1)S(1)} %collective-permute-done.14), channel_id=1, source_target_pairs={{0,1},{1,2},{2,3},{3,4},{4,5},{5,6},{6,7},{7,8},{8,9},{9,10},{10,1... | collective-permute-start | bytes 1769480 | tf_op jit(solution)/shard_map/ppermute | solution.py:75
  232.1 38.0 %collective-permute-start = (bf16[3,8,8,1536]{3,2,1,0:T(8,128)(2,1)}, bf16[3,8,8,1536]{3,2,1,0:T(8,128)(2,1)S(1)}, u32[]{:S(2)}, u32[]{:S(2)}) collective-permute-start(bf16[3,8,8,1536]{3,2,1,0:T(8,128)(2,1)} %slice.55), channel_id=1, source_target_pairs={{0,1},{1,2},{2,3},{3,4},{4,5},{5,6},{6,7},{7,8},{8,9},{9,10},{10,1... | collective-permute-start | bytes 1769480 | tf_op jit(solution)/shard_map/ppermute | solution.py:14
  254.7 31.3 %collective-permute-start.16 = (bf16[96,3072]{1,0:T(8,128)(2,1)}, bf16[96,3072]{1,0:T(8,128)(2,1)}, u32[]{:S(2)}, u32[]{:S(2)}) collective-permute-start(bf16[96,3072]{1,0:T(8,128)(2,1)} %collective-permute-done.15), channel_id=1, source_target_pairs={{0,1},{1,2},{2,3},{3,4},{4,5},{5,6},{6,7},{7,8},{8,9},{9,10},{10,1... | collective-permute-start | bytes 1769480 | tf_op jit(solution)/shard_map/ppermute | solution.py:75
  270.8 19.9 %copy-start.25 = (bf16[96,3072]{1,0:T(8,128)(2,1)S(1)}, bf16[96,3072]{1,0:T(8,128)(2,1)}, u32[]{:S(2)}) copy-start(bf16[96,3072]{1,0:T(8,128)(2,1)} %copy-done.24) | copy-start | bytes 1769476
  272.5 17.4 %copy-start.28 = (bf16[96,3072]{1,0:T(8,128)(2,1)S(1)}, bf16[96,3072]{1,0:T(8,128)(2,1)}, u32[]{:S(2)}) copy-start(bf16[96,3072]{1,0:T(8,128)(2,1)} %copy-done.27) | copy-start | bytes 1769476
  272.5 21.1 %copy-start.23 = (bf16[96,3072]{1,0:T(8,128)(2,1)S(1)}, bf16[96,3072]{1,0:T(8,128)(2,1)}, u32[]{:S(2)}) copy-start(bf16[96,3072]{1,0:T(8,128)(2,1)} %copy-done.22) | copy-start | bytes 1769476
  272.5 22.0 %copy-start.21 = (bf16[96,3072]{1,0:T(8,128)(2,1)S(1)}, bf16[96,3072]{1,0:T(8,128)(2,1)}, u32[]{:S(2)}) copy-start(bf16[96,3072]{1,0:T(8,128)(2,1)} %copy-done.20) | copy-start | bytes 1769476
  275.3 20.1 %copy-start.19 = (bf16[96,3072]{1,0:T(8,128)(2,1)S(1)}, bf16[96,3072]{1,0:T(8,128)(2,1)}, u32[]{:S(2)}) copy-start(bf16[96,3072]{1,0:T(8,128)(2,1)} %copy-done.18) | copy-start | bytes 1769476
  275.3 21.0 %copy-start.17 = (bf16[96,3072]{1,0:T(8,128)(2,1)S(1)}, bf16[96,3072]{1,0:T(8,128)(2,1)}, u32[]{:S(2)}) copy-start(bf16[96,3072]{1,0:T(8,128)(2,1)} %copy-done.16) | copy-start | bytes 1769476
  287.9 9.2 %copy-start.15 = (bf16[96,3072]{1,0:T(8,128)(2,1)S(1)}, bf16[96,3072]{1,0:T(8,128)(2,1)}, u32[]{:S(2)}) copy-start(bf16[96,3072]{1,0:T(8,128)(2,1)} %copy-done.14) | copy-start | bytes 1769476
  289.9 8.1 %copy-start.13 = (bf16[96,3072]{1,0:T(8,128)(2,1)S(1)}, bf16[96,3072]{1,0:T(8,128)(2,1)}, u32[]{:S(2)}) copy-start(bf16[96,3072]{1,0:T(8,128)(2,1)} %copy-done.12) | copy-start | bytes 1769476
  290.8 8.1 %copy-start.11 = (bf16[96,3072]{1,0:T(8,128)(2,1)S(1)}, bf16[96,3072]{1,0:T(8,128)(2,1)}, u32[]{:S(2)}) copy-start(bf16[96,3072]{1,0:T(8,128)(2,1)} %copy-done.10) | copy-start | bytes 1769476
  291.7 8.1 %copy-start.9 = (bf16[96,3072]{1,0:T(8,128)(2,1)S(1)}, bf16[96,3072]{1,0:T(8,128)(2,1)}, u32[]{:S(2)}) copy-start(bf16[96,3072]{1,0:T(8,128)(2,1)} %copy-done.8) | copy-start | bytes 1769476
  293.7 7.0 %copy-start.7 = (bf16[96,3072]{1,0:T(8,128)(2,1)S(1)}, bf16[96,3072]{1,0:T(8,128)(2,1)}, u32[]{:S(2)}) copy-start(bf16[96,3072]{1,0:T(8,128)(2,1)} %copy-done.6) | copy-start | bytes 1769476
  294.5 7.1 %copy-start.5 = (bf16[96,3072]{1,0:T(8,128)(2,1)S(1)}, bf16[96,3072]{1,0:T(8,128)(2,1)}, u32[]{:S(2)}) copy-start(bf16[96,3072]{1,0:T(8,128)(2,1)} %copy-done.4) | copy-start | bytes 1769476
  295.4 7.1 %copy-start.3 = (bf16[96,3072]{1,0:T(8,128)(2,1)S(1)}, bf16[96,3072]{1,0:T(8,128)(2,1)}, u32[]{:S(2)}) copy-start(bf16[96,3072]{1,0:T(8,128)(2,1)} %param.16) | copy-start | bytes 1769476
  298.9 9.2 %copy-start.26 = (bf16[96,3072]{1,0:T(8,128)(2,1)S(1)}, bf16[96,3072]{1,0:T(8,128)(2,1)}, u32[]{:S(2)}) copy-start(bf16[96,3072]{1,0:T(8,128)(2,1)} %copy-done.24) | copy-start | bytes 1769476
  329.0 2.9 copy-start.29
  335.3 6.1 %copy-start.33 = (f32[3,1536]{1,0:T(4,128)S(1)}, f32[3,1536]{1,0:T(4,128)}, u32[]{:S(2)}) copy-start(f32[3,1536]{1,0:T(4,128)} %get-tuple-element.13) | copy-start | bytes 55300
  336.2 4.5 %collective-permute-start.1 = (bf16[3,8,8,768]{3,1,0,2:T(8,128)(2,1)S(1)}, bf16[3,8,8,768]{3,1,0,2:T(8,128)(2,1)S(1)}, u32[]{:S(2)}, u32[]{:S(2)}) collective-permute-start(bf16[3,8,8,768]{3,1,0,2:T(8,128)(2,1)S(1)} %slice.59), channel_id=1, source_target_pairs={{0,15},{1,0},{2,1},{3,2},{4,3},{5,4},{6,5},{7,6},{8,7},{9,8},{10,9... | collective-permute-start | bytes 884744 | tf_op jit(solution)/shard_map/ppermute | solution.py:14
  340.8 4.0 %copy-start.31 = (f32[3,1536]{1,0:T(4,128)S(1)}, f32[3,1536]{1,0:T(4,128)}, u32[]{:S(2)}) copy-start(f32[3,1536]{1,0:T(4,128)} %get-tuple-element.9) | copy-start | bytes 55300
  340.8 4.0 %copy-start.32 = (f32[3,1536]{1,0:T(4,128)S(1)}, f32[3,1536]{1,0:T(4,128)}, u32[]{:S(2)}) copy-start(f32[3,1536]{1,0:T(4,128)} %get-tuple-element.10) | copy-start | bytes 55300
  345.5 24.0 %copy-start.30 = (f32[3,1536]{1,0:T(4,128)S(1)}, f32[3,1536]{1,0:T(4,128)}, u32[]{:S(2)}) copy-start(f32[3,1536]{1,0:T(4,128)} %get-tuple-element.8) | copy-start | bytes 55300
  345.5 27.1 %copy-start.1 = (bf16[32,6,1536]{2,0,1:T(8,128)(2,1)S(1)}, bf16[32,6,1536]{2,0,1:T(8,128)(2,1)}, u32[]{:S(2)}) copy-start(bf16[32,6,1536]{2,0,1:T(8,128)(2,1)} %param.12) | copy-start | bytes 1769476
Sparse Core Ops, SparseCore 0:
  9.6 81.8 all-gather.3
  93.8 46.5 all-gather.5
  179.9 97.0 all-gather.7
